TPU v7x, 32 devices: a whole 2x2x4 slice. The times are simulated.
32 devices in a mesh: af: 4 (over y, x), sa: 8 (over z, core).
Axes of the slice: x: 2, y: 2, z: 4, core: 2. Of those that a mesh axis runs over, the one named last changes fastest.
Arguments:
- data_real: bfloat16 [64, 512, 512], P('af', 'sa'), may hold values from -0.5 to 0.5
- data_imaginary: bfloat16 [64, 512, 512], P('af', 'sa'), may hold values from -0.5 to 0.5
- wavelet_real: float32 [64], P('af'), may hold values from -2.5 to 2.5
- wavelet_imaginary: float32 [64], P('af'), may hold values from -2.5 to 2.5
- primaries_real: float32 [64, 512, 512], P('af', 'sa'), may hold values from -3 to 3
- primaries_imaginary: float32 [64, 512, 512], P('af', 'sa'), may hold values from -3 to 3
Outputs:
- updated_real: float32 [64, 512, 512], P('af', 'sa')
- updated_imaginary: float32 [64, 512, 512], P('af', 'sa')
- misfit: float32 [2], replicated
All inputs are finite; a program needn't handle non-finite values.
Results may differ from a plain program's by a relative error of at most 0.0018.
Values may be sent and summed in bfloat16 or wider, within the bound.
A program may use at most 128 MiB of HBM per device.

v0:
```python
import math
import jax
import jax.numpy as jnp
from jax import lax
from jax.sharding import PartitionSpec as P

N = 512
F = 64
ITERS = 2
STEP_LENGTH = 0.02
THRESHOLD = 0.25


def fourier_tables(row_index, col_index):
    phase = row_index[:, None] * col_index[None, :] % F
    angle = phase.astype(jnp.float32) * (2.0 * math.pi / F)
    factor = 1.0 / math.sqrt(F)
    return (jnp.cos(angle) * factor, jnp.sin(angle) * factor)


def highest(left, right):
    return jnp.dot(left, right, precision=lax.Precision.HIGHEST, preferred_element_type=jnp.float32)


def stacked(part_real, part_imaginary):
    return jnp.concatenate(
        [part_real.astype(jnp.bfloat16), part_imaginary.astype(jnp.bfloat16)], axis=1
    )


def shrink(values):
    return values - jnp.clip(values, -THRESHOLD, THRESHOLD)


def on_device(
    data_real, data_imaginary, wavelet_real, wavelet_imaginary, primaries_real, primaries_imaginary
):
    row_count = data_real.shape[1]
    wave_real = wavelet_real[:, None, None]
    wave_imaginary = wavelet_imaginary[:, None, None]
    current_real = primaries_real
    current_imaginary = primaries_imaginary
    own_real = data_real.astype(jnp.float32)
    own_imaginary = data_imaginary.astype(jnp.float32)
    whole_real, whole_imaginary = (
        lax.all_gather(data_real, "sa", axis=1, tiled=True),
        lax.all_gather(data_imaginary, "sa", axis=1, tiled=True),
    )
    local_sums = []
    for iteration in range(ITERS):
        left_rows = stacked(current_real, current_imaginary)
        product_real = jnp.einsum(
            "frk,fkc->frc", left_rows, whole_real, preferred_element_type=jnp.float32
        )
        product_imaginary = jnp.einsum(
            "frk,fkc->frc", left_rows, whole_imaginary, preferred_element_type=jnp.float32
        )
        forward_real = product_real[:, :row_count] - product_imaginary[:, row_count:]
        forward_imaginary = product_imaginary[:, :row_count] + product_real[:, row_count:]
        error_real = (
            own_real
            + forward_real
            - (wave_real * current_real - wave_imaginary * current_imaginary)
        )
        error_imaginary = (
            own_imaginary
            + forward_imaginary
            - (wave_real * current_imaginary + wave_imaginary * current_real)
        )
        local_sum = jnp.sum(error_real * error_real) + jnp.sum(error_imaginary * error_imaginary)
        local_sums.append(local_sum)
        error_rows = stacked(error_real, error_imaginary)
        with_real = jnp.einsum(
            "frk,fjk->frj", error_rows, whole_real, preferred_element_type=jnp.float32
        )
        with_imaginary = jnp.einsum(
            "frk,fjk->frj", error_rows, whole_imaginary, preferred_element_type=jnp.float32
        )
        back_real = with_real[:, :row_count] + with_imaginary[:, row_count:]
        back_imaginary = with_real[:, row_count:] - with_imaginary[:, :row_count]
        gradient_real = wave_real * error_real + wave_imaginary * error_imaginary - back_real
        gradient_imaginary = (
            wave_real * error_imaginary - wave_imaginary * error_real - back_imaginary
        )
        stepped_real = current_real + STEP_LENGTH * gradient_real
        stepped_imaginary = current_imaginary + STEP_LENGTH * gradient_imaginary
        trace_real, trace_imaginary = (
            lax.all_to_all(stepped_real, "af", split_axis=2, concat_axis=0, tiled=True),
            lax.all_to_all(stepped_imaginary, "af", split_axis=2, concat_axis=0, tiled=True),
        )
        block_shape = trace_real.shape
        flat_real = trace_real.reshape(F, -1)
        flat_imaginary = trace_imaginary.reshape(F, -1)
        every_index = jnp.arange(F, dtype=jnp.int32)
        cosine, sine = fourier_tables(every_index, every_index)
        time_real = highest(cosine, flat_real) - highest(sine, flat_imaginary)
        time_imaginary = highest(sine, flat_real) + highest(cosine, flat_imaginary)
        shrunk_real = shrink(time_real)
        shrunk_imaginary = shrink(time_imaginary)
        freq_real = (highest(cosine, shrunk_real) + highest(sine, shrunk_imaginary)).reshape(
            block_shape
        )
        freq_imaginary = (highest(cosine, shrunk_imaginary) - highest(sine, shrunk_real)).reshape(
            block_shape
        )
        current_real, current_imaginary = (
            lax.all_to_all(freq_real, "af", split_axis=0, concat_axis=2, tiled=True),
            lax.all_to_all(freq_imaginary, "af", split_axis=0, concat_axis=2, tiled=True),
        )
    totals = lax.psum(jnp.stack(local_sums), ("af", "sa"))
    misfit = totals / (F * N * N)
    return (current_real, current_imaginary, misfit)


def solution(mesh):
    in_specs = (
        P("af", "sa", None),
        P("af", "sa", None),
        P("af"),
        P("af"),
        P("af", "sa", None),
        P("af", "sa", None),
    )
    out_specs = (P("af", "sa", None), P("af", "sa", None), P())
    return jax.shard_map(
        on_device, mesh=mesh, in_specs=in_specs, out_specs=out_specs, check_vma=False
    )
```

profile of v0, /device:TPU:0, one launch (start us, length us, event | category | flops | bytes accessed | tf_op | source)
XLA Modules:
  0.0 607.2 jit_solution(6934212573473681621)
XLA Ops:
  12.5 81.9 %all-gather.5.cloned.1.call-done = bf16[16,512,512]{2,1,0:T(8,128)(2,1)} async-done(((bf16[16,64,512]{2,1,0:T(8,128)(2,1)}), bf16[16,512,512]{2,1,0:T(8,128)(2,1)}) %all-gather.5.cloned.1.call-update) | async-done | bytes 8388624 | tf_op jit(solution)/shard_map/all_gather | solution.py:47
  94.4 7.3 %fusion.46 = f32[16,128,512]{2,1,0:T(8,128)} fusion(bf16[16,512,512]{2,1,0:T(8,128)(2,1)} %all-gather.5.cloned.1.call-done, bf16[16,64,512]{2,1,0:T(8,128)(2,1)} %convert_element_type.67, bf16[16,64,512]{2,1,0:T(8,128)(2,1)} %convert_element_type.66), kind=kOutput, calls=%fused_computation.88 | convolution fusion | flops 1077936128 | bytes 14680064 | tf_op jit(solution)/shard_map/frk,fkc->frc/dot_general | solution.py:55
  101.6 74.9 %all-gather.3.cloned.1.call-done = bf16[16,512,512]{2,1,0:T(8,128)(2,1)} async-done(((bf16[16,64,512]{2,1,0:T(8,128)(2,1)}), bf16[16,512,512]{2,1,0:T(8,128)(2,1)}) %all-gather.3.cloned.1.call-update) | async-done | bytes 8388624 | tf_op jit(solution)/shard_map/all_gather | solution.py:46
  176.5 5.4 fusion.47
  189.1 6.8 %fusion.44 = f32[16,128,512]{2,1,0:T(8,128)} fusion(bf16[16,512,512]{2,1,0:T(8,128)(2,1)S(1)} %bitcast.119, bf16[16,64,512]{2,1,0:T(8,128)(2,1)} %convert_element_type.70, bf16[16,64,512]{2,1,0:T(8,128)(2,1)} %convert_element_type.69), kind=kOutput, calls=%fused_computation.86 | convolution fusion | flops 1077936128 | bytes 14680064 | tf_op jit(solution)/shard_map/frk,fjk->frj/dot_general | solution.py:76
  195.9 6.5 %fusion.45 = f32[16,128,512]{2,1,0:T(8,128)} fusion(bf16[16,512,512]{2,1,0:T(8,128)(2,1)S(1)} %bitcast.123, bf16[16,64,512]{2,1,0:T(8,128)(2,1)} %convert_element_type.70, bf16[16,64,512]{2,1,0:T(8,128)(2,1)} %convert_element_type.69), kind=kOutput, calls=%fused_computation.87 | convolution fusion | flops 1077936128 | bytes 14680064 | tf_op jit(solution)/shard_map/frk,fjk->frj/dot_general | solution.py:73
  202.5 5.8 fusion.24
  208.3 4.9 copy.19
  213.2 5.5 reshape.44
  222.3 4.9 copy.21
  227.1 5.5 reshape.46
  232.6 15.1 %all-to-all-done = f32[4,1,131072]{2,1,0:T(1,128)S(1)} async-done(((f32[4,1,131072]{2,1,0:T(1,128)}), f32[4,1,131072]{2,1,0:T(1,128)S(1)}, u32[]{:S(2)}, u32[]{:S(2)}) %all-to-all-start) | async-done | bytes 2097184 | tf_op jit(solution)/shard_map/all_to_all | solution.py:88
  249.1 4.9 all-to-all-start.1
  254.5 7.6 %reduce = f32[4,131072]{1,0:T(4,128)S(1)} reduce(f32[4,1,131072]{2,1,0:T(1,128)} %copy-done.27, f32[]{:T(128)} %broadcast.92), dimensions={1}, to_apply=%all_to_all.96.reduce_sub_computation | reduce | bytes 4194308 | tf_op jit(solution)/shard_map/all_to_all | solution.py:88
  278.7 7.6 %reduce.1 = f32[4,131072]{1,0:T(4,128)S(1)} reduce(f32[4,1,131072]{2,1,0:T(1,128)} %all-to-all-done.1, f32[]{:T(128)} %broadcast.92), dimensions={1}, to_apply=%all_to_all.99.reduce_sub_computation | reduce | bytes 4194308 | tf_op jit(solution)/shard_map/all_to_all | solution.py:89
  293.8 4.9 clamp_subtract_fusion.2
  319.4 16.8 %all-to-all-done.3 = f32[64,64,128]{2,1,0:T(8,128)S(1)} async-done(((f32[64,64,128]{2,1,0:T(8,128)}), f32[64,64,128]{2,1,0:T(8,128)S(1)}, u32[]{:S(2)}, u32[]{:S(2)}) %all-to-all-start.3) | async-done | bytes 2097184 | tf_op jit(solution)/shard_map/all_to_all | solution.py:108
  341.8 23.3 %all-to-all-done.2 = f32[64,64,128]{2,1,0:T(8,128)} async-done(((f32[64,64,128]{2,1,0:T(8,128)}), f32[64,64,128]{2,1,0:T(8,128)}, u32[]{:S(2)}, u32[]{:S(2)}) %all-to-all-start.2) | async-done | bytes 2097184 | tf_op jit(solution)/shard_map/all_to_all | solution.py:107
  367.1 4.9 fusion.42
  381.0 6.4 %fusion.40 = f32[16,128,512]{2,1,0:T(8,128)} fusion(bf16[16,512,512]{2,1,0:T(8,128)(2,1)S(1)} %bitcast.121, bf16[16,64,512]{2,1,0:T(8,128)(2,1)} %convert_element_type.74, bf16[16,64,512]{2,1,0:T(8,128)(2,1)} %convert_element_type.73), kind=kOutput, calls=%fused_computation.82 | convolution fusion | flops 1077936128 | bytes 14680064 | tf_op jit(solution)/shard_map/frk,fjk->frj/dot_general | solution.py:76
  387.4 6.5 %fusion.41 = f32[16,128,512]{2,1,0:T(8,128)} fusion(bf16[16,512,512]{2,1,0:T(8,128)(2,1)S(1)} %bitcast.125, bf16[16,64,512]{2,1,0:T(8,128)(2,1)} %convert_element_type.74, bf16[16,64,512]{2,1,0:T(8,128)(2,1)} %convert_element_type.73), kind=kOutput, calls=%fused_computation.83 | convolution fusion | flops 1077936128 | bytes 14680064 | tf_op jit(solution)/shard_map/frk,fjk->frj/dot_general | solution.py:73
  393.9 5.1 bitcast_add_fusion
  399.0 4.9 copy.25
  403.8 5.5 reshape.48
  412.9 4.9 copy.27
  417.8 5.5 reshape.50
  423.3 13.9 %all-to-all-done.4 = f32[4,1,131072]{2,1,0:T(1,128)S(1)} async-done(((f32[4,1,131072]{2,1,0:T(1,128)}), f32[4,1,131072]{2,1,0:T(1,128)S(1)}, u32[]{:S(2)}, u32[]{:S(2)}) %all-to-all-start.4) | async-done | bytes 2097184 | tf_op jit(solution)/shard_map/all_to_all | solution.py:88
  443.3 7.6 %reduce.2 = f32[4,131072]{1,0:T(4,128)S(1)} reduce(f32[4,1,131072]{2,1,0:T(1,128)} %copy-done.28, f32[]{:T(128)} %broadcast.92), dimensions={1}, to_apply=%all_to_all.110.reduce_sub_computation | reduce | bytes 4194308 | tf_op jit(solution)/shard_map/all_to_all | solution.py:88
  467.7 7.6 %reduce.3 = f32[4,131072]{1,0:T(4,128)S(1)} reduce(f32[4,1,131072]{2,1,0:T(1,128)} %all-to-all-done.5, f32[]{:T(128)} %broadcast.92), dimensions={1}, to_apply=%all_to_all.113.reduce_sub_computation | reduce | bytes 4194308 | tf_op jit(solution)/shard_map/all_to_all | solution.py:89
  482.5 4.9 clamp_subtract_fusion
  507.5 18.5 %all-to-all-done.6 = f32[64,64,128]{2,1,0:T(8,128)} async-done(((f32[64,64,128]{2,1,0:T(8,128)}), f32[64,64,128]{2,1,0:T(8,128)}, u32[]{:S(2)}, u32[]{:S(2)}) %all-to-all-start.6) | async-done | bytes 2097184 | tf_op jit(solution)/shard_map/all_to_all | solution.py:107
  532.2 54.3 %psum.7 = f32[2]{0:T(128)S(1)} all-reduce(f32[2]{0:T(128)S(1)} %pad_maximum_fusion.12), channel_id=1, replica_groups=mesh['af'=4,'sa'=8] {'af','sa'}, use_global_device_ids=true, to_apply=%region_4.5 | all-reduce | flops 2 | bytes 16 | tf_op jit(solution)/shard_map/psum | solution.py:110
  (140 shorter events, 149.9 us)
Async XLA Ops:
  7.2 87.2 %all-gather.5.cloned.1.call-start = ((), (), s32[]{:S(2)}) async-start(), calls=%async_computation.9 | async-start | bytes 9437184 | tf_op jit(solution)/shard_map/all_gather | solution.py:47
  7.9 168.6 %all-gather.3.cloned.1.call-start = ((), (), s32[]{:S(2)}) async-start(), calls=%async_computation.8 | async-start | bytes 9437184 | tf_op jit(solution)/shard_map/all_gather | solution.py:46
  101.6 80.3 %copy-start.29 = (f32[16]{0:T(128)S(1)}, f32[16]{0:T(128)}, u32[]{:S(2)}) copy-start(f32[16]{0:T(128)} %param.9) | copy-start | bytes 196
  101.6 80.4 %copy-start.30 = (f32[16]{0:T(128)S(1)}, f32[16]{0:T(128)}, u32[]{:S(2)}) copy-start(f32[16]{0:T(128)} %param.8) | copy-start | bytes 196
  176.5 5.5 copy-start
  176.5 5.9 copy-start.9
  176.5 6.1 %copy-start.21 = (bf16[16,64,512]{2,1,0:T(8,128)(2,1)S(1)}, bf16[16,64,512]{2,1,0:T(8,128)(2,1)}, u32[]{:S(2)}) copy-start(bf16[16,64,512]{2,1,0:T(8,128)(2,1)} %param.7) | copy-start | bytes 3145732
  176.5 6.4 %copy-start.23 = (bf16[16,64,512]{2,1,0:T(8,128)(2,1)S(1)}, bf16[16,64,512]{2,1,0:T(8,128)(2,1)}, u32[]{:S(2)}) copy-start(bf16[16,64,512]{2,1,0:T(8,128)(2,1)} %param.6) | copy-start | bytes 3145732
  176.5 12.5 %slice-start = ((s8[8388608]{0:T(1024)(128)(4,1)}), s8[4194304]{0:T(1024)(128)(4,1)S(1)}, s32[]{:S(2)}) async-start(s8[8388608]{0:T(1024)(128)(4,1)} %bitcast.118), calls=%async_computation.10 | async-start | bytes 8388608
  182.9 6.1 %slice-start.1 = ((s8[8388608]{0:T(1024)(128)(4,1)}), s8[4194304]{0:T(1024)(128)(4,1)S(1)}, s32[]{:S(2)}) async-start(s8[8388608]{0:T(1024)(128)(4,1)} %bitcast.118), calls=%async_computation.11 | async-start | bytes 8388608
  187.9 8.0 %slice-start.4 = ((s8[8388608]{0:T(1024)(128)(4,1)}), s8[4194304]{0:T(1024)(128)(4,1)S(1)}, s32[]{:S(2)}) async-start(s8[8388608]{0:T(1024)(128)(4,1)} %bitcast.122), calls=%async_computation.14 | async-start | bytes 8388608
  189.0 6.8 %slice-start.5 = ((s8[8388608]{0:T(1024)(128)(4,1)}), s8[4194304]{0:T(1024)(128)(4,1)S(1)}, s32[]{:S(2)}) async-start(s8[8388608]{0:T(1024)(128)(4,1)} %bitcast.122), calls=%async_computation.15 | async-start | bytes 8388608
  195.9 6.6 %copy-start.10 = (f32[16,64,512]{2,1,0:T(8,128)S(1)}, f32[16,64,512]{2,1,0:T(8,128)}, u32[]{:S(2)}) copy-start(f32[16,64,512]{2,1,0:T(8,128)} %param.10) | copy-start | bytes 6291460
  195.9 6.6 %copy-start.16 = (f32[16,64,512]{2,1,0:T(8,128)S(1)}, f32[16,64,512]{2,1,0:T(8,128)}, u32[]{:S(2)}) copy-start(f32[16,64,512]{2,1,0:T(8,128)} %copy-done.15) | copy-start | bytes 6291460
  195.9 6.5 %copy-start.18 = (f32[16,64,512]{2,1,0:T(8,128)S(1)}, f32[16,64,512]{2,1,0:T(8,128)}, u32[]{:S(2)}) copy-start(f32[16,64,512]{2,1,0:T(8,128)} %copy-done.17) | copy-start | bytes 6291460
  218.7 29.1 %all-to-all-start = ((f32[4,1,131072]{2,1,0:T(1,128)}), f32[4,1,131072]{2,1,0:T(1,128)S(1)}, u32[]{:S(2)}, u32[]{:S(2)}) async-start(f32[4,1,131072]{2,1,0:T(1,128)} %reshape.44), calls=%async_computation | async-start | bytes 4194304 | tf_op jit(solution)/shard_map/all_to_all | solution.py:88
  249.1 29.6 %all-to-all-start.1 = ((f32[4,1,131072]{2,1,0:T(1,128)}), f32[4,1,131072]{2,1,0:T(1,128)}, u32[]{:S(2)}, u32[]{:S(2)}) async-start(f32[4,1,131072]{2,1,0:T(1,128)} %reshape.46), calls=%async_computation.1 | async-start | bytes 4194304 | tf_op jit(solution)/shard_map/all_to_all | solution.py:89
  302.0 6.0 copy-start.7
  308.0 28.2 %all-to-all-start.3 = ((f32[64,64,128]{2,1,0:T(8,128)}), f32[64,64,128]{2,1,0:T(8,128)S(1)}, u32[]{:S(2)}, u32[]{:S(2)}) async-start(f32[64,64,128]{2,1,0:T(8,128)} %bitcast.150), calls=%async_computation.3 | async-start | bytes 4194304 | tf_op jit(solution)/shard_map/all_to_all | solution.py:108
  336.2 28.9 %all-to-all-start.2 = ((f32[64,64,128]{2,1,0:T(8,128)}), f32[64,64,128]{2,1,0:T(8,128)}, u32[]{:S(2)}, u32[]{:S(2)}) async-start(f32[64,64,128]{2,1,0:T(8,128)} %bitcast.152), calls=%async_computation.2 | async-start | bytes 4194304 | tf_op jit(solution)/shard_map/all_to_all | solution.py:107
  365.1 6.9 %slice-start.6 = ((s8[8388608]{0:T(1024)(128)(4,1)}), s8[4194304]{0:T(1024)(128)(4,1)S(1)}, s32[]{:S(2)}) async-start(s8[8388608]{0:T(1024)(128)(4,1)} %bitcast.124), calls=%async_computation.16 | async-start | bytes 8388608
  367.0 5.1 slice-start.7
  372.1 8.9 %slice-start.2 = ((s8[8388608]{0:T(1024)(128)(4,1)}), s8[4194304]{0:T(1024)(128)(4,1)S(1)}, s32[]{:S(2)}) async-start(s8[8388608]{0:T(1024)(128)(4,1)} %bitcast.120), calls=%async_computation.12 | async-start | bytes 8388608
  373.7 7.4 %slice-start.3 = ((s8[8388608]{0:T(1024)(128)(4,1)}), s8[4194304]{0:T(1024)(128)(4,1)S(1)}, s32[]{:S(2)}) async-start(s8[8388608]{0:T(1024)(128)(4,1)} %bitcast.120), calls=%async_computation.13 | async-start | bytes 8388608
  387.4 6.5 %copy-start.12 = (f32[16,64,512]{2,1,0:T(8,128)S(1)}, f32[16,64,512]{2,1,0:T(8,128)}, u32[]{:S(2)}) copy-start(f32[16,64,512]{2,1,0:T(8,128)} %copy-done.11) | copy-start | bytes 6291460
  387.4 6.5 %copy-start.14 = (f32[16,64,512]{2,1,0:T(8,128)S(1)}, f32[16,64,512]{2,1,0:T(8,128)}, u32[]{:S(2)}) copy-start(f32[16,64,512]{2,1,0:T(8,128)} %copy-done.13) | copy-start | bytes 6291460
  387.4 6.5 %copy-start.19 = (f32[16,128,512]{2,1,0:T(8,128)S(1)}, f32[16,128,512]{2,1,0:T(8,128)}, u32[]{:S(2)}) copy-start(f32[16,128,512]{2,1,0:T(8,128)} %fusion.40) | copy-start | bytes 12582916
  409.3 28.0 %all-to-all-start.4 = ((f32[4,1,131072]{2,1,0:T(1,128)}), f32[4,1,131072]{2,1,0:T(1,128)S(1)}, u32[]{:S(2)}, u32[]{:S(2)}) async-start(f32[4,1,131072]{2,1,0:T(1,128)} %reshape.48), calls=%async_computation.4 | async-start | bytes 4194304 | tf_op jit(solution)/shard_map/all_to_all | solution.py:88
  438.6 29.1 %all-to-all-start.5 = ((f32[4,1,131072]{2,1,0:T(1,128)}), f32[4,1,131072]{2,1,0:T(1,128)}, u32[]{:S(2)}, u32[]{:S(2)}) async-start(f32[4,1,131072]{2,1,0:T(1,128)} %reshape.50), calls=%async_computation.5 | async-start | bytes 4194304 | tf_op jit(solution)/shard_map/all_to_all | solution.py:89
  487.5 5.4 copy-start.3
  496.7 29.3 %all-to-all-start.6 = ((f32[64,64,128]{2,1,0:T(8,128)}), f32[64,64,128]{2,1,0:T(8,128)}, u32[]{:S(2)}, u32[]{:S(2)}) async-start(f32[64,64,128]{2,1,0:T(8,128)} %bitcast.151), calls=%async_computation.6 | async-start | bytes 4194304 | tf_op jit(solution)/shard_map/all_to_all | solution.py:107
  526.0 68.3 %all-to-all-start.7 = ((f32[64,64,128]{2,1,0:T(8,128)}), f32[64,64,128]{2,1,0:T(8,128)S(1)}, u32[]{:S(2)}, u32[]{:S(2)}) async-start(f32[64,64,128]{2,1,0:T(8,128)} %bitcast.43), calls=%async_computation.7 | async-start | bytes 4194304 | tf_op jit(solution)/shard_map/all_to_all | solution.py:108
  (17 other events, 44.6 us)
Sparse Core Ops, SparseCore 0:
  9.6 84.7 all-gather.4
  96.0 80.5 all-gather.2
where the time goes:
time: 617 us; the launch traced here: 607 us
  waiting for transfers between devices  247 us (40%)
  local copies, waits for them, and re-layouts  101 us (16%)
  matrix products  97.7 us (16%)
  other arithmetic  56.9 us (9%)
  blocking collectives  54.3 us (9%)
  starting transfers between devices  33.6 us (5%)
  between operations  17.2 us (3%)
    all_gather x1, waiting for transfers between devices, on_device(): lax.all_gather(data_imaginary, 'sa', axis=1, tiled=True)  81.9 us
    all_gather x1, waiting for transfers between devices, on_device(): lax.all_gather(data_real, 'sa', axis=1, tiled=True)  74.9 us
    psum x1, blocking collectives, on_device(): totals = lax.psum(jnp.stack(local_sums), ('af', 'sa'))  54.3 us
    dot_general x16, matrix products, highest(): jnp.dot(left, right, precision=lax.Precision.HIGHEST, preferred_element_t...  52.7 us
    unnamed x90, local copies, waits for them, and re-layouts  51.6 us
    all_to_all x2, waiting for transfers between devices, on_device(): lax.all_to_all(freq_real, 'af', split_axis=0, concat_axis=2, tiled=True)  41.8 us
    all_to_all x2, waiting for transfers between devices, on_device(): lax.all_to_all(stepped_real, 'af', split_axis=2, concat_axis=0, tiled=True)  29.1 us
    all_to_all x2, waiting for transfers between devices, on_device(): lax.all_to_all(freq_imaginary, 'af', split_axis=0, concat_axis=2, tiled=T...  16.8 us
  transfers between devices with their start and end apart: 10, of which 9 were waited for; matrix products, arithmetic and copies ran while one was open for 16% of the time, Pallas kernels for 0%

commit v1 on v0

--- a/solution.py
+++ b/solution.py
@@ -85,7 +85,12 @@
         stepped_real = current_real + STEP_LENGTH * gradient_real
         stepped_imaginary = current_imaginary + STEP_LENGTH * gradient_imaginary
         trace_real, trace_imaginary = (
-            lax.all_to_all(stepped_real, "af", split_axis=2, concat_axis=0, tiled=True),
+            jnp.concatenate(
+                lax.all_to_all(
+                    jnp.stack(jnp.split(stepped_real, lax.axis_size("af"), axis=2)), "af", 0, 0
+                ),
+                axis=0,
+            ),
             lax.all_to_all(stepped_imaginary, "af", split_axis=2, concat_axis=0, tiled=True),
         )
         block_shape = trace_real.shape

time: 617 us -> 595 us (0.964)
  local copies, waits for them, and re-layouts: 101 us -> 63.4 us
  waiting for transfers between devices: 247 us -> 277 us
  other arithmetic: 56.9 us -> 44.2 us
    all_to_all x2, waiting for transfers between devices: 1.08 us -> 30.9 us  [on_device(): lax.all_to_all(stepped_imaginary, 'af', split_axis=2, concat_axis=0, tile...]
    unnamed x90 -> x82, local copies, waits for them, and re-layouts: 51.6 us -> 30.1 us
    all_to_all x2 -> x0, other arithmetic: 15.2 us -> none  [on_device(): lax.all_to_all(stepped_real, 'af', split_axis=2, concat_axis=0, tiled=True)]
    add x2 -> x0, local copies, waits for them, and re-layouts: 9.72 us -> none  [on_device(): stepped_real = current_real + STEP_LENGTH * gradient_real]
    all_to_all x3 -> x0, local copies, waits for them, and re-layouts: 7.19 us -> none  [on_device(): lax.all_to_all(stepped_real, 'af', split_axis=2, concat_axis=0, tiled=True)]
  transfers between devices with their start and end apart: 10 -> 10, of which waited for: 9 -> 9; matrix products, arithmetic and copies ran while one was open for 16% -> 12% of each run, Pallas kernels for 0% -> 0%
where the time goes in v1:
time: 595 us; the launch traced here: 587 us
  waiting for transfers between devices  277 us (47%)
  matrix products  97.7 us (16%)
  local copies, waits for them, and re-layouts  63.4 us (11%)
  blocking collectives  54.1 us (9%)
  other arithmetic  44.2 us (7%)
  starting transfers between devices  33.4 us (6%)
  between operations  17.4 us (3%)
    all_gather x1, waiting for transfers between devices, on_device(): lax.all_gather(data_imaginary, 'sa', axis=1, tiled=True)  81.9 us
    all_gather x1, waiting for transfers between devices, on_device(): lax.all_gather(data_real, 'sa', axis=1, tiled=True)  74.9 us
    psum x1, blocking collectives, on_device(): totals = lax.psum(jnp.stack(local_sums), ('af', 'sa'))  54.1 us
    dot_general x16, matrix products, highest(): jnp.dot(left, right, precision=lax.Precision.HIGHEST, preferred_element_t...  52.7 us
    all_to_all x2, waiting for transfers between devices, on_device(): lax.all_to_all(freq_real, 'af', split_axis=0, concat_axis=2, tiled=True)  41.7 us
    all_to_all x2, waiting for transfers between devices, on_device(): lax.all_to_all(stepped_imaginary, 'af', split_axis=2, concat_axis=0, tile...  30.9 us
    unnamed x82, local copies, waits for them, and re-layouts  30.1 us
    all_to_all x2, waiting for transfers between devices, on_device(): lax.all_to_all(jnp.stack(jnp.split(stepped_real, lax.axis_size('af'), axi...  29.1 us
  transfers between devices with their start and end apart: 10, of which 9 were waited for; matrix products, arithmetic and copies ran while one was open for 12% of the time, Pallas kernels for 0%

profile of v1, /device:TPU:0, one launch (start us, length us, event | category | flops | bytes accessed | tf_op | source)
XLA Modules:
  0.0 586.8 jit_solution(15857278290643605927)
XLA Ops:
  12.5 81.9 %all-gather.5.cloned.1.call-done = bf16[16,512,512]{2,1,0:T(8,128)(2,1)} async-done(((bf16[16,64,512]{2,1,0:T(8,128)(2,1)}), bf16[16,512,512]{2,1,0:T(8,128)(2,1)}) %all-gather.5.cloned.1.call-update) | async-done | bytes 8388624 | tf_op jit(solution)/shard_map/all_gather | solution.py:47
  94.4 7.3 %fusion.46 = f32[16,128,512]{2,1,0:T(8,128)} fusion(bf16[16,512,512]{2,1,0:T(8,128)(2,1)} %all-gather.5.cloned.1.call-done, bf16[16,64,512]{2,1,0:T(8,128)(2,1)} %convert_element_type.67, bf16[16,64,512]{2,1,0:T(8,128)(2,1)} %convert_element_type.66), kind=kOutput, calls=%fused_computation.90 | convolution fusion | flops 1077936128 | bytes 14680064 | tf_op jit(solution)/shard_map/frk,fkc->frc/dot_general | solution.py:55
  101.6 74.9 %all-gather.3.cloned.1.call-done = bf16[16,512,512]{2,1,0:T(8,128)(2,1)} async-done(((bf16[16,64,512]{2,1,0:T(8,128)(2,1)}), bf16[16,512,512]{2,1,0:T(8,128)(2,1)}) %all-gather.3.cloned.1.call-update) | async-done | bytes 8388624 | tf_op jit(solution)/shard_map/all_gather | solution.py:46
  176.5 5.4 fusion.47
  189.1 6.8 %fusion.44 = f32[16,128,512]{2,1,0:T(8,128)} fusion(bf16[16,512,512]{2,1,0:T(8,128)(2,1)S(1)} %bitcast.127, bf16[16,64,512]{2,1,0:T(8,128)(2,1)} %convert_element_type.70, bf16[16,64,512]{2,1,0:T(8,128)(2,1)} %convert_element_type.69), kind=kOutput, calls=%fused_computation.88 | convolution fusion | flops 1077936128 | bytes 14680064 | tf_op jit(solution)/shard_map/frk,fjk->frj/dot_general | solution.py:76
  195.9 6.5 %fusion.45 = f32[16,128,512]{2,1,0:T(8,128)} fusion(bf16[16,512,512]{2,1,0:T(8,128)(2,1)S(1)} %bitcast.131, bf16[16,64,512]{2,1,0:T(8,128)(2,1)} %convert_element_type.70, bf16[16,64,512]{2,1,0:T(8,128)(2,1)} %convert_element_type.69), kind=kOutput, calls=%fused_computation.89 | convolution fusion | flops 1077936128 | bytes 14680064 | tf_op jit(solution)/shard_map/frk,fjk->frj/dot_general | solution.py:73
  202.5 5.5 fusion.24
  213.4 4.9 copy.17
  218.2 5.5 reshape.34
  223.7 15.1 %all-to-all-done = f32[4,16,64,128]{3,2,1,0:T(8,128)S(1)} async-done(((f32[4,16,64,128]{3,2,1,0:T(8,128)}), f32[4,16,64,128]{3,2,1,0:T(8,128)S(1)}, u32[]{:S(2)}, u32[]{:S(2)}) %all-to-all-start) | async-done | bytes 2097184 | tf_op jit(solution)/shard_map/all_to_all | solution.py:89
  238.9 4.6 all-to-all-start.1
  252.3 15.7 %all-to-all-done.1 = f32[4,1,131072]{2,1,0:T(1,128)} async-done(((f32[4,1,131072]{2,1,0:T(1,128)}), f32[4,1,131072]{2,1,0:T(1,128)}, u32[]{:S(2)}, u32[]{:S(2)}) %all-to-all-start.1) | async-done | bytes 2097184 | tf_op jit(solution)/shard_map/all_to_all | solution.py:94
  268.6 7.8 %reduce = f32[4,131072]{1,0:T(4,128)S(1)} reduce(f32[4,1,131072]{2,1,0:T(1,128)} %all-to-all-done.1, f32[]{:T(128)} %broadcast.92), dimensions={1}, to_apply=%all_to_all.81.reduce_sub_computation | reduce | bytes 4194308 | tf_op jit(solution)/shard_map/all_to_all | solution.py:94
  283.8 4.9 clamp_subtract_fusion.2
  309.4 16.7 %all-to-all-done.3 = f32[64,64,128]{2,1,0:T(8,128)S(1)} async-done(((f32[64,64,128]{2,1,0:T(8,128)}), f32[64,64,128]{2,1,0:T(8,128)S(1)}, u32[]{:S(2)}, u32[]{:S(2)}) %all-to-all-start.3) | async-done | bytes 2097184 | tf_op jit(solution)/shard_map/all_to_all | solution.py:113
  326.1 4.4 all-to-all-start.2
  331.8 23.3 %all-to-all-done.2 = f32[64,64,128]{2,1,0:T(8,128)} async-done(((f32[64,64,128]{2,1,0:T(8,128)}), f32[64,64,128]{2,1,0:T(8,128)}, u32[]{:S(2)}, u32[]{:S(2)}) %all-to-all-start.2) | async-done | bytes 2097184 | tf_op jit(solution)/shard_map/all_to_all | solution.py:112
  357.0 4.9 fusion.42
  371.0 6.4 %fusion.40 = f32[16,128,512]{2,1,0:T(8,128)} fusion(bf16[16,512,512]{2,1,0:T(8,128)(2,1)S(1)} %bitcast.129, bf16[16,64,512]{2,1,0:T(8,128)(2,1)} %convert_element_type.74, bf16[16,64,512]{2,1,0:T(8,128)(2,1)} %convert_element_type.73), kind=kOutput, calls=%fused_computation.84 | convolution fusion | flops 1077936128 | bytes 14680064 | tf_op jit(solution)/shard_map/frk,fjk->frj/dot_general | solution.py:76
  377.4 6.5 %fusion.41 = f32[16,128,512]{2,1,0:T(8,128)} fusion(bf16[16,512,512]{2,1,0:T(8,128)(2,1)S(1)} %bitcast.133, bf16[16,64,512]{2,1,0:T(8,128)(2,1)} %convert_element_type.74, bf16[16,64,512]{2,1,0:T(8,128)(2,1)} %convert_element_type.73), kind=kOutput, calls=%fused_computation.85 | convolution fusion | flops 1077936128 | bytes 14680064 | tf_op jit(solution)/shard_map/frk,fjk->frj/dot_general | solution.py:73
  383.9 4.7 bitcast_add_fusion
  394.0 4.9 copy.21
  398.8 5.5 reshape.36
  404.3 14.0 %all-to-all-done.4 = f32[4,16,64,128]{3,2,1,0:T(8,128)S(1)} async-done(((f32[4,16,64,128]{3,2,1,0:T(8,128)}), f32[4,16,64,128]{3,2,1,0:T(8,128)S(1)}, u32[]{:S(2)}, u32[]{:S(2)}) %all-to-all-start.4) | async-done | bytes 2097184 | tf_op jit(solution)/shard_map/all_to_all | solution.py:89
  418.3 4.9 all-to-all-start.5
  427.6 4.4 fusion.8
  432.0 15.2 %all-to-all-done.5 = f32[4,1,131072]{2,1,0:T(1,128)} async-done(((f32[4,1,131072]{2,1,0:T(1,128)}), f32[4,1,131072]{2,1,0:T(1,128)}, u32[]{:S(2)}, u32[]{:S(2)}) %all-to-all-start.5) | async-done | bytes 2097184 | tf_op jit(solution)/shard_map/all_to_all | solution.py:94
  447.2 7.8 %reduce.1 = f32[4,131072]{1,0:T(4,128)S(1)} reduce(f32[4,1,131072]{2,1,0:T(1,128)} %all-to-all-done.5, f32[]{:T(128)} %broadcast.92), dimensions={1}, to_apply=%all_to_all.93.reduce_sub_computation | reduce | bytes 4194308 | tf_op jit(solution)/shard_map/all_to_all | solution.py:94
  462.2 5.0 clamp_subtract_fusion
  476.4 4.8 all-to-all-start.6
  487.2 18.4 %all-to-all-done.6 = f32[64,64,128]{2,1,0:T(8,128)} async-done(((f32[64,64,128]{2,1,0:T(8,128)}), f32[64,64,128]{2,1,0:T(8,128)}, u32[]{:S(2)}, u32[]{:S(2)}) %all-to-all-start.6) | async-done | bytes 2097184 | tf_op jit(solution)/shard_map/all_to_all | solution.py:112
  511.9 54.1 %psum.7 = f32[2]{0:T(128)S(1)} all-reduce(f32[2]{0:T(128)S(1)} %pad_maximum_fusion.14), channel_id=1, replica_groups=mesh['af'=4,'sa'=8] {'af','sa'}, use_global_device_ids=true, to_apply=%region_4.5 | all-reduce | flops 2 | bytes 16 | tf_op jit(solution)/shard_map/psum | solution.py:115
  (130 shorter events, 116.9 us)
Async XLA Ops:
  7.2 87.2 %all-gather.5.cloned.1.call-start = ((), (), s32[]{:S(2)}) async-start(), calls=%async_computation.9 | async-start | bytes 9437184 | tf_op jit(solution)/shard_map/all_gather | solution.py:47
  7.9 168.6 %all-gather.3.cloned.1.call-start = ((), (), s32[]{:S(2)}) async-start(), calls=%async_computation.8 | async-start | bytes 9437184 | tf_op jit(solution)/shard_map/all_gather | solution.py:46
  101.6 80.3 %copy-start.27 = (f32[16]{0:T(128)S(1)}, f32[16]{0:T(128)}, u32[]{:S(2)}) copy-start(f32[16]{0:T(128)} %param.9) | copy-start | bytes 196
  101.6 80.3 %copy-start.28 = (f32[16]{0:T(128)S(1)}, f32[16]{0:T(128)}, u32[]{:S(2)}) copy-start(f32[16]{0:T(128)} %param.8) | copy-start | bytes 196
  176.5 5.5 copy-start
  176.5 5.9 %copy-start.9 = (f32[16,64,512]{2,1,0:T(8,128)S(1)}, f32[16,64,512]{2,1,0:T(8,128)}, u32[]{:S(2)}) copy-start(f32[16,64,512]{2,1,0:T(8,128)} %param.10) | copy-start | bytes 6291460
  176.5 6.1 %copy-start.21 = (bf16[16,64,512]{2,1,0:T(8,128)(2,1)S(1)}, bf16[16,64,512]{2,1,0:T(8,128)(2,1)}, u32[]{:S(2)}) copy-start(bf16[16,64,512]{2,1,0:T(8,128)(2,1)} %param.7) | copy-start | bytes 3145732
  176.5 6.4 %copy-start.23 = (bf16[16,64,512]{2,1,0:T(8,128)(2,1)S(1)}, bf16[16,64,512]{2,1,0:T(8,128)(2,1)}, u32[]{:S(2)}) copy-start(bf16[16,64,512]{2,1,0:T(8,128)(2,1)} %param.6) | copy-start | bytes 3145732
  176.5 12.5 %slice-start = ((s8[8388608]{0:T(1024)(128)(4,1)}), s8[4194304]{0:T(1024)(128)(4,1)S(1)}, s32[]{:S(2)}) async-start(s8[8388608]{0:T(1024)(128)(4,1)} %bitcast.126), calls=%async_computation.10 | async-start | bytes 8388608
  182.9 6.1 %slice-start.1 = ((s8[8388608]{0:T(1024)(128)(4,1)}), s8[4194304]{0:T(1024)(128)(4,1)S(1)}, s32[]{:S(2)}) async-start(s8[8388608]{0:T(1024)(128)(4,1)} %bitcast.126), calls=%async_computation.11 | async-start | bytes 8388608
  187.9 8.0 %slice-start.4 = ((s8[8388608]{0:T(1024)(128)(4,1)}), s8[4194304]{0:T(1024)(128)(4,1)S(1)}, s32[]{:S(2)}) async-start(s8[8388608]{0:T(1024)(128)(4,1)} %bitcast.130), calls=%async_computation.14 | async-start | bytes 8388608
  189.1 6.9 %slice-start.5 = ((s8[8388608]{0:T(1024)(128)(4,1)}), s8[4194304]{0:T(1024)(128)(4,1)S(1)}, s32[]{:S(2)}) async-start(s8[8388608]{0:T(1024)(128)(4,1)} %bitcast.130), calls=%async_computation.15 | async-start | bytes 8388608
  195.9 6.6 %copy-start.10 = (f32[16,64,512]{2,1,0:T(8,128)S(1)}, f32[16,64,512]{2,1,0:T(8,128)}, u32[]{:S(2)}) copy-start(f32[16,64,512]{2,1,0:T(8,128)} %param.10) | copy-start | bytes 6291460
  195.9 6.6 %copy-start.16 = (f32[16,64,512]{2,1,0:T(8,128)S(1)}, f32[16,64,512]{2,1,0:T(8,128)}, u32[]{:S(2)}) copy-start(f32[16,64,512]{2,1,0:T(8,128)} %copy-done.15) | copy-start | bytes 6291460
  195.9 6.6 %copy-start.18 = (f32[16,64,512]{2,1,0:T(8,128)S(1)}, f32[16,64,512]{2,1,0:T(8,128)}, u32[]{:S(2)}) copy-start(f32[16,64,512]{2,1,0:T(8,128)} %copy-done.17) | copy-start | bytes 6291460
  209.7 29.1 %all-to-all-start = ((f32[4,16,64,128]{3,2,1,0:T(8,128)}), f32[4,16,64,128]{3,2,1,0:T(8,128)S(1)}, u32[]{:S(2)}, u32[]{:S(2)}) async-start(f32[4,16,64,128]{3,2,1,0:T(8,128)} %pad_maximum_fusion.2), calls=%async_computation | async-start | bytes 4194304 | tf_op jit(solution)/shard_map/all_to_all | solution.py:89
  238.9 29.1 %all-to-all-start.1 = ((f32[4,1,131072]{2,1,0:T(1,128)}), f32[4,1,131072]{2,1,0:T(1,128)}, u32[]{:S(2)}, u32[]{:S(2)}) async-start(f32[4,1,131072]{2,1,0:T(1,128)} %reshape.34), calls=%async_computation.1 | async-start | bytes 4194304 | tf_op jit(solution)/shard_map/all_to_all | solution.py:94
  292.0 6.0 %copy-start.7 = (f32[64,8192]{1,0:T(8,128)}, f32[64,8192]{1,0:T(8,128)S(1)}, u32[]{:S(2)}) copy-start(f32[64,8192]{1,0:T(8,128)S(1)} %clamp_subtract_fusion.3) | copy-start | bytes 6291460
  298.0 28.1 %all-to-all-start.3 = ((f32[64,64,128]{2,1,0:T(8,128)}), f32[64,64,128]{2,1,0:T(8,128)S(1)}, u32[]{:S(2)}, u32[]{:S(2)}) async-start(f32[64,64,128]{2,1,0:T(8,128)} %bitcast.154), calls=%async_computation.3 | async-start | bytes 4194304 | tf_op jit(solution)/shard_map/all_to_all | solution.py:113
  326.1 28.9 %all-to-all-start.2 = ((f32[64,64,128]{2,1,0:T(8,128)}), f32[64,64,128]{2,1,0:T(8,128)}, u32[]{:S(2)}, u32[]{:S(2)}) async-start(f32[64,64,128]{2,1,0:T(8,128)} %bitcast.156), calls=%async_computation.2 | async-start | bytes 4194304 | tf_op jit(solution)/shard_map/all_to_all | solution.py:112
  355.1 6.8 %slice-start.6 = ((s8[8388608]{0:T(1024)(128)(4,1)}), s8[4194304]{0:T(1024)(128)(4,1)S(1)}, s32[]{:S(2)}) async-start(s8[8388608]{0:T(1024)(128)(4,1)} %bitcast.132), calls=%async_computation.16 | async-start | bytes 8388608
  357.0 5.1 slice-start.7
  362.1 9.0 %slice-start.2 = ((s8[8388608]{0:T(1024)(128)(4,1)}), s8[4194304]{0:T(1024)(128)(4,1)S(1)}, s32[]{:S(2)}) async-start(s8[8388608]{0:T(1024)(128)(4,1)} %bitcast.128), calls=%async_computation.12 | async-start | bytes 8388608
  363.6 7.4 %slice-start.3 = ((s8[8388608]{0:T(1024)(128)(4,1)}), s8[4194304]{0:T(1024)(128)(4,1)S(1)}, s32[]{:S(2)}) async-start(s8[8388608]{0:T(1024)(128)(4,1)} %bitcast.128), calls=%async_computation.13 | async-start | bytes 8388608
  377.4 6.5 %copy-start.12 = (f32[16,64,512]{2,1,0:T(8,128)S(1)}, f32[16,64,512]{2,1,0:T(8,128)}, u32[]{:S(2)}) copy-start(f32[16,64,512]{2,1,0:T(8,128)} %copy-done.11) | copy-start | bytes 6291460
  377.4 6.5 %copy-start.14 = (f32[16,64,512]{2,1,0:T(8,128)S(1)}, f32[16,64,512]{2,1,0:T(8,128)}, u32[]{:S(2)}) copy-start(f32[16,64,512]{2,1,0:T(8,128)} %copy-done.13) | copy-start | bytes 6291460
  377.4 6.5 %copy-start.19 = (f32[16,128,512]{2,1,0:T(8,128)S(1)}, f32[16,128,512]{2,1,0:T(8,128)}, u32[]{:S(2)}) copy-start(f32[16,128,512]{2,1,0:T(8,128)} %fusion.40) | copy-start | bytes 12582916
  390.3 28.0 %all-to-all-start.4 = ((f32[4,16,64,128]{3,2,1,0:T(8,128)}), f32[4,16,64,128]{3,2,1,0:T(8,128)S(1)}, u32[]{:S(2)}, u32[]{:S(2)}) async-start(f32[4,16,64,128]{3,2,1,0:T(8,128)} %pad_maximum_fusion.5), calls=%async_computation.4 | async-start | bytes 4194304 | tf_op jit(solution)/shard_map/all_to_all | solution.py:89
  418.3 28.9 %all-to-all-start.5 = ((f32[4,1,131072]{2,1,0:T(1,128)}), f32[4,1,131072]{2,1,0:T(1,128)}, u32[]{:S(2)}, u32[]{:S(2)}) async-start(f32[4,1,131072]{2,1,0:T(1,128)} %reshape.36), calls=%async_computation.5 | async-start | bytes 4194304 | tf_op jit(solution)/shard_map/all_to_all | solution.py:94
  467.2 5.4 copy-start.3
  476.4 29.2 %all-to-all-start.6 = ((f32[64,64,128]{2,1,0:T(8,128)}), f32[64,64,128]{2,1,0:T(8,128)}, u32[]{:S(2)}, u32[]{:S(2)}) async-start(f32[64,64,128]{2,1,0:T(8,128)} %bitcast.155), calls=%async_computation.6 | async-start | bytes 4194304 | tf_op jit(solution)/shard_map/all_to_all | solution.py:112
  505.7 68.3 %all-to-all-start.7 = ((f32[64,64,128]{2,1,0:T(8,128)}), f32[64,64,128]{2,1,0:T(8,128)S(1)}, u32[]{:S(2)}, u32[]{:S(2)}) async-start(f32[64,64,128]{2,1,0:T(8,128)} %bitcast.47), calls=%async_computation.7 | async-start | bytes 4194304 | tf_op jit(solution)/shard_map/all_to_all | solution.py:113
  (15 other events, 42.0 us)
Sparse Core Ops, SparseCore 0:
  9.6 84.7 all-gather.4
  96.0 80.5 all-gather.2
